TPU v7x, 32 devices: a whole 2x2x4 slice. The times are simulated.
32 devices in a mesh: north: 8 (over y, x, core), deep: 4 (over z).
Axes of the slice: x: 2, y: 2, z: 4, core: 2. Of those that a mesh axis runs over, the one named last changes fastest.
Arguments:
- velocity: float32 [4, 128, 64, 256], P(None, None, 'north', 'deep'), may hold values from -6 to 6
- coupling: float32 [4, 4], replicated, may hold values from -4 to 4
- symbol_x: float32 [128], replicated, may hold values from 0.3 to 3
- symbol_y: float32 [64], replicated, may hold values from 0.3 to 3
- symbol_z: float32 [256], replicated, may hold values from 0.3 to 3
Outputs:
- spectrum: float32 [4, 128, 64, 256], P(None, 'north', 'deep')
All inputs are finite; a program needn't handle non-finite values.
Results may differ from a plain program's by a relative error of at most 0.00007.
Values sent between devices are 32-bit elements; how exact they have to be, the bound alone decides.
A program may use at most 128 MiB of HBM per device.

v0:
```python
import jax
import jax.numpy as jnp
from jax import lax
from jax.sharding import PartitionSpec as P


def basis_table(count):
    rank = jnp.arange(count)
    angle = (
        jnp.pi
        / (count + 1)
        * ((rank[:, None] + 1) * (rank[None, :] + 1) % (2 * count + 2)).astype(jnp.float32)
    )
    return jnp.sin(angle) * (2.0 / (count + 1)) ** 0.5


def along_dim(values, dim):
    moved = jnp.tensordot(
        values, basis_table(values.shape[dim]), axes=([dim], [0]), precision=lax.Precision.HIGHEST
    )
    return jnp.moveaxis(moved, -1, dim)


def on_device(velocity, coupling, symbol_x, symbol_y, symbol_z):
    part_values = velocity
    part_values = along_dim(part_values, 1)
    part_values = lax.all_to_all(part_values, "north", split_axis=1, concat_axis=2, tiled=True)
    part_values = along_dim(part_values, 2)
    block_values = part_values
    block_values = lax.all_to_all(block_values, "deep", split_axis=2, concat_axis=3, tiled=True)
    block_values = along_dim(block_values, 3)
    share_x = block_values.shape[1]
    part_x = lax.dynamic_slice_in_dim(symbol_x, lax.axis_index("north") * share_x, share_x)
    share_y = block_values.shape[2]
    part_y = lax.dynamic_slice_in_dim(symbol_y, lax.axis_index("deep") * share_y, share_y)
    symbol = part_x[:, None, None] + part_y[None, :, None] + symbol_z[None, None, :]
    weight_xyz = 1.0 / (1.0 + symbol)
    mixed_fields = jnp.einsum(
        "ab,bxyz->axyz", coupling, block_values, precision=lax.Precision.HIGHEST
    )
    block_values = weight_xyz * block_values + (1.0 - weight_xyz) * mixed_fields
    return block_values


def solution(mesh):
    placed = (P(None, None, "north", "deep"), P(), P(), P(), P())
    return jax.shard_map(
        on_device,
        mesh=mesh,
        in_specs=placed,
        out_specs=P(None, "north", "deep", None),
        check_vma=False,
    )
```

profile of v0, /device:TPU:2, one launch (start us, length us, event | category | flops | bytes accessed | tf_op | source)
XLA Modules:
  0.0 93.1 jit_solution(7834806281157115720)
XLA Ops:
  0.0 0.0 copy-start
  0.0 1.2 %copy-done = f32[4,128,8,64]{1,3,2,0:T(8,128)S(1)} copy-done((f32[4,128,8,64]{1,3,2,0:T(8,128)S(1)}, f32[4,128,8,64]{1,3,2,0:T(8,128)}, u32[]{:S(2)}) %copy-start) | copy-done | bytes 1048600
  1.2 2.3 %fusion.29 = f32[128,2048]{0,1} fusion(f32[128,2048]{0,1:T(8,128)S(1)} %bitcast.42, s32[128]{0:T(128)S(1)} %iota_add_fusion.2), kind=kOutput, calls=%fused_computation.32 | convolution fusion | flops 402817024 | bytes 2097664
  3.5 3.1 %copy.17 = f32[4,128,8,64]{3,2,0,1:T(8,128)S(1)} copy(f32[4,128,8,64]{1,3,2,0:T(8,128)} %bitcast.47) | data formatting | bytes 2097152 | tf_op jit(solution)/shard_map/transpose | solution.py:21
  6.6 2.1 %reshape.72 = f32[8,1,32768]{2,1,0:T(1,128)} reshape(f32[128,4,8,64]{3,2,1,0:T(8,128)S(1)} %bitcast.44) | data formatting | bytes 2097152
  8.7 4.3 %all-to-all-start = ((f32[8,1,32768]{2,1,0:T(1,128)}), f32[8,1,32768]{2,1,0:T(1,128)S(1)}, u32[]{:S(2)}, u32[]{:S(2)}) async-start(f32[8,1,32768]{2,1,0:T(1,128)} %reshape.72), calls=%async_computation | async-start | bytes 2097152 | tf_op jit(solution)/shard_map/all_to_all | solution.py:27
  12.9 13.9 %all-to-all-done = f32[8,1,32768]{2,1,0:T(1,128)S(1)} async-done(((f32[8,1,32768]{2,1,0:T(1,128)}), f32[8,1,32768]{2,1,0:T(1,128)S(1)}, u32[]{:S(2)}, u32[]{:S(2)}) %all-to-all-start) | async-done | bytes 1048608 | tf_op jit(solution)/shard_map/all_to_all | solution.py:27
  26.8 0.6 broadcast.101
  27.4 4.5 %reduce = f32[8,32768]{1,0:T(8,128)} reduce(f32[8,1,32768]{2,1,0:T(1,128)S(1)} %all-to-all-done, f32[]{:T(128)} %broadcast.101), dimensions={1}, to_apply=%all_to_all.26.reduce_sub_computation | reduce | bytes 2097156 | tf_op jit(solution)/shard_map/all_to_all | solution.py:27
  31.9 2.1 %reshape.73 = f32[128,4,8,64]{3,2,1,0:T(8,128)S(1)} reshape(f32[8,32768]{1,0:T(8,128)} %reduce) | data formatting | bytes 2097152
  33.9 4.8 %fusion.3 = f32[4,16,64,64]{2,3,1,0:T(8,128)} fusion(f32[4,16,8,8,64]{4,3,0,1,2:T(8,128)S(1)} %bitcast.43, s32[64]{0:T(128)S(1)} %iota_add_fusion.1), kind=kOutput, calls=%fused_computation.3 | convolution fusion | flops 201367552 | bytes 2097408 | tf_op jit(solution)/shard_map/dot_general | solution.py:18
  38.7 3.1 %copy.21 = f32[4,16,64,64]{3,1,0,2:T(8,128)S(1)} copy(f32[4,16,64,64]{2,3,1,0:T(8,128)} %fusion.3) | data formatting | bytes 2097152 | tf_op jit(solution)/shard_map/transpose | solution.py:21
  41.9 0.0 copy-start.4
  41.9 0.0 copy-start.5
  41.9 0.0 copy-start.3
  41.9 2.4 %reshape.74 = f32[4,1,65536]{2,1,0:T(1,128)} reshape(f32[64,4,16,64]{3,2,1,0:T(8,128)S(1)} %bitcast.45) | data formatting | bytes 2097152
  44.3 4.9 %all-to-all-start.1 = ((f32[4,1,65536]{2,1,0:T(1,128)}), f32[4,1,65536]{2,1,0:T(1,128)S(1)}, u32[]{:S(2)}, u32[]{:S(2)}) async-start(f32[4,1,65536]{2,1,0:T(1,128)} %reshape.74), calls=%async_computation.1 | async-start | bytes 2097152 | tf_op jit(solution)/shard_map/all_to_all | solution.py:30
  49.2 0.0 copy-done.4
  49.2 0.1 dynamic_slice.7
  49.2 0.0 copy-done.5
  49.2 0.1 dynamic_slice.6
  49.3 0.1 broadcast_add_fusion
  49.4 0.0 copy-done.3
  49.4 0.8 add_divide_fusion
  50.2 24.9 %all-to-all-done.1 = f32[4,1,65536]{2,1,0:T(1,128)S(1)} async-done(((f32[4,1,65536]{2,1,0:T(1,128)}), f32[4,1,65536]{2,1,0:T(1,128)S(1)}, u32[]{:S(2)}, u32[]{:S(2)}) %all-to-all-start.1) | async-done | bytes 1048608 | tf_op jit(solution)/shard_map/all_to_all | solution.py:30
  75.1 4.6 %reduce.1 = f32[4,65536]{1,0:T(4,128)} reduce(f32[4,1,65536]{2,1,0:T(1,128)S(1)} %all-to-all-done.1, f32[]{:T(128)} %broadcast.101), dimensions={1}, to_apply=%all_to_all.30.reduce_sub_computation | reduce | bytes 2097156 | tf_op jit(solution)/shard_map/all_to_all | solution.py:30
  79.7 2.2 %reshape.75 = f32[64,4,16,64]{3,2,1,0:T(8,128)S(1)} reshape(f32[4,65536]{1,0:T(4,128)} %reduce.1) | data formatting | bytes 2097152
  82.0 2.7 %copy.23 = f32[4,16,16,4,64]{4,3,2,1,0:T(4,128)} copy(f32[4,16,16,4,64]{4,1,0,2,3:T(8,128)S(1)} %bitcast.46) | data formatting | bytes 2097152 | tf_op jit(solution)/shard_map/all_to_all | solution.py:30
  84.7 2.5 %all_to_all.33 = f32[4,16,16,256]{3,2,1,0:T(8,128)S(1)} reshape(f32[4,16,16,4,64]{4,3,2,1,0:T(4,128)} %copy.23) | data formatting | bytes 2097152 | tf_op jit(solution)/shard_map/all_to_all | solution.py:30
  87.2 2.1 %fusion.13 = f32[4,16,16,256]{3,2,1,0:T(8,128)S(1)} fusion(f32[4,16,16,256]{3,2,1,0:T(8,128)S(1)} %all_to_all.33, s32[256]{0:T(256)S(1)} %iota_add_fusion), kind=kOutput, calls=%fused_computation.14 | convolution fusion | flops 805961728 | bytes 2098176 | tf_op jit(solution)/shard_map/dot_general | solution.py:18
  89.3 2.5 %fusion.6 = f32[16,16,256,4]{2,3,1,0:T(4,128)S(1)} fusion(f32[4,16,16,256]{3,2,1,0:T(8,128)S(1)} %fusion.13, f32[4,4]{1,0:T(4,128)S(1)} %copy-done.2), kind=kOutput, calls=%fused_computation.6 | convolution fusion | flops 12582912 | bytes 2097216 | tf_op jit(solution)/shard_map/ab,bxyz->axyz/dot_general | solution.py:38
  91.8 1.3 %bitcast_add_fusion = f32[4,16,16,256]{3,2,1,0:T(8,128)} fusion(f32[16,16,256,4]{2,3,1,0:T(4,128)S(1)} %fusion.6, f32[4,16,16,256]{3,2,1,0:T(8,128)S(1)} %fusion.13, f32[16,16,256]{2,1,0:T(8,128)S(1)} %copy-done.1, f32[16,16,256]{2,1,0:T(8,128)S(1)} %get-tuple-element.5), kind=kLoop, calls=%fused_computation.4 | loop fusion | flops 786432 | bytes 3670016 | tf_op jit(solution)/shard_map/add | solution.py:41
  (7 shorter events, 0.0 us)
Async XLA Ops:
  0.0 1.2 %copy-start = (f32[4,128,8,64]{1,3,2,0:T(8,128)S(1)}, f32[4,128,8,64]{1,3,2,0:T(8,128)}, u32[]{:S(2)}) copy-start(f32[4,128,8,64]{1,3,2,0:T(8,128)} %param.5) | copy-start | bytes 3145732
  8.7 18.1 %all-to-all-start = ((f32[8,1,32768]{2,1,0:T(1,128)}), f32[8,1,32768]{2,1,0:T(1,128)S(1)}, u32[]{:S(2)}, u32[]{:S(2)}) async-start(f32[8,1,32768]{2,1,0:T(1,128)} %reshape.72), calls=%async_computation | async-start | bytes 2097152 | tf_op jit(solution)/shard_map/all_to_all | solution.py:27
  41.9 7.3 %copy-start.4 = (f32[64]{0:T(128)S(1)}, f32[64]{0:T(128)}, u32[]{:S(2)}) copy-start(f32[64]{0:T(128)} %param.8) | copy-start | bytes 772
  41.9 7.4 %copy-start.5 = (f32[128]{0:T(128)S(1)}, f32[128]{0:T(128)}, u32[]{:S(2)}) copy-start(f32[128]{0:T(128)} %param.7) | copy-start | bytes 1540
  41.9 7.5 %copy-start.3 = (f32[256]{0:T(256)S(1)}, f32[256]{0:T(256)}, u32[]{:S(2)}) copy-start(f32[256]{0:T(256)} %param.9) | copy-start | bytes 3076
  44.3 30.8 %all-to-all-start.1 = ((f32[4,1,65536]{2,1,0:T(1,128)}), f32[4,1,65536]{2,1,0:T(1,128)S(1)}, u32[]{:S(2)}, u32[]{:S(2)}) async-start(f32[4,1,65536]{2,1,0:T(1,128)} %reshape.74), calls=%async_computation.1 | async-start | bytes 2097152 | tf_op jit(solution)/shard_map/all_to_all | solution.py:30
  84.7 4.6 %copy-start.2 = (f32[4,4]{1,0:T(4,128)S(1)}, f32[4,4]{1,0:T(4,128)}, u32[]{:S(2)}) copy-start(f32[4,4]{1,0:T(4,128)} %param.6) | copy-start | bytes 196
  87.2 4.6 %copy-start.1 = (f32[16,16,256]{2,1,0:T(8,128)S(1)}, f32[16,16,256]{2,1,0:T(8,128)}, u32[]{:S(2)}) copy-start(f32[16,16,256]{2,1,0:T(8,128)} %get-tuple-element.6) | copy-start | bytes 786436
where the time goes:
time: 93.5 us; the launch traced here: 93.1 us
  waiting for transfers between devices  38.8 us (41%)
  local copies, waits for them, and re-layouts  22.1 us (24%)
  matrix products  11.6 us (12%)
  other arithmetic  11.3 us (12%)
  starting transfers between devices  9.12 us (10%)
    all_to_all x1, waiting for transfers between devices, on_device(): lax.all_to_all(block_values, 'deep', split_axis=2, concat_axis=3, tiled=T...  24.9 us
    all_to_all x1, waiting for transfers between devices, on_device(): lax.all_to_all(part_values, 'north', split_axis=1, concat_axis=2, tiled=T...  13.9 us
    unnamed x16, local copies, waits for them, and re-layouts  10.1 us
    dot_general x2, matrix products, along_dim(): jnp.tensordot(values, basis_table(values.shape[dim]), axes=([dim], [0]),...  6.89 us
    transpose x2, local copies, waits for them, and re-layouts, along_dim(): return jnp.moveaxis(moved, -1, dim)  6.15 us
    all_to_all x2, local copies, waits for them, and re-layouts, on_device(): lax.all_to_all(block_values, 'deep', split_axis=2, concat_axis=3, tiled=T...  5.19 us
    all_to_all x1, starting transfers between devices, on_device(): lax.all_to_all(block_values, 'deep', split_axis=2, concat_axis=3, tiled=T...  4.87 us
    all_to_all x1, other arithmetic, on_device(): lax.all_to_all(block_values, 'deep', split_axis=2, concat_axis=3, tiled=T...  4.63 us
  transfers between devices with their start and end apart: 2, of which 2 were waited for; matrix products, arithmetic and copies ran while one was open for 1% of the time, Pallas kernels for 0%

commit v1 on v0

--- a/solution.py
+++ b/solution.py
@@ -24,7 +24,12 @@
 def on_device(velocity, coupling, symbol_x, symbol_y, symbol_z):
     part_values = velocity
     part_values = along_dim(part_values, 1)
-    part_values = lax.all_to_all(part_values, "north", split_axis=1, concat_axis=2, tiled=True)
+    part_values = jnp.concatenate(
+        lax.all_to_all(
+            jnp.stack(jnp.split(part_values, lax.axis_size("north"), axis=1)), "north", 0, 0
+        ),
+        axis=2,
+    )
     part_values = along_dim(part_values, 2)
     block_values = part_values
     block_values = lax.all_to_all(block_values, "deep", split_axis=2, concat_axis=3, tiled=True)

time: 93.5 us -> 113 us (1.21)
  local copies, waits for them, and re-layouts: 22.1 us -> 42.6 us
    another operation x0 -> x10, local copies, waits for them, and re-layouts: none -> 19.5 us  [on_device(): jnp.stack(jnp.split(part_values, lax.axis_size('north'), axis=1))]
    unnamed x16 -> x29, local copies, waits for them, and re-layouts: 10.1 us -> 14.1 us
    transpose x2 -> x1, local copies, waits for them, and re-layouts: 6.15 us -> 3.1 us  [along_dim(): return jnp.moveaxis(moved, -1, dim)]
where the time goes in v1:
time: 113 us
  local copies, waits for them, and re-layouts  42.6 us (38%)
  waiting for transfers between devices  38.8 us (34%)
  other arithmetic  11.3 us (10%)
  matrix products  10.7 us (9%)
  starting transfers between devices  9.12 us (8%)
    all_to_all x1, waiting for transfers between devices, on_device(): lax.all_to_all(block_values, 'deep', split_axis=2, concat_axis=3, tiled=T...  24.9 us
    another operation x10, local copies, waits for them, and re-layouts, on_device(): jnp.stack(jnp.split(part_values, lax.axis_size('north'), axis=1))  19.5 us
    unnamed x29, local copies, waits for them, and re-layouts  14.1 us
    all_to_all x1, waiting for transfers between devices, on_device(): lax.all_to_all(jnp.stack(jnp.split(part_values, lax.axis_size('north'), a...  13.9 us
    dot_general x2, matrix products, along_dim(): jnp.tensordot(values, basis_table(values.shape[dim]), axes=([dim], [0]),...  6.89 us
    all_to_all x2, local copies, waits for them, and re-layouts, on_device(): lax.all_to_all(block_values, 'deep', split_axis=2, concat_axis=3, tiled=T...  5.19 us
    all_to_all x1, starting transfers between devices, on_device(): lax.all_to_all(block_values, 'deep', split_axis=2, concat_axis=3, tiled=T...  4.87 us
    all_to_all x1, other arithmetic, on_device(): lax.all_to_all(block_values, 'deep', split_axis=2, concat_axis=3, tiled=T...  4.64 us
  transfers between devices with their start and end apart: 2, of which 2 were waited for; matrix products, arithmetic and copies ran while one was open for 1% of the time, Pallas kernels for 0%

profile of v1, /device:TPU:2, one launch (start us, length us, event | category | flops | bytes accessed | tf_op | source)
XLA Modules:
  0.0 112.7 jit_solution(17592133481644340484)
XLA Ops:
  0.0 1.2 %copy-done = f32[4,128,8,64]{1,3,2,0:T(8,128)S(1)} copy-done((f32[4,128,8,64]{1,3,2,0:T(8,128)S(1)}, f32[4,128,8,64]{1,3,2,0:T(8,128)}, u32[]{:S(2)}) %copy-start) | copy-done | bytes 1048600
  1.2 1.3 %fusion.29 = f32[128,2048]{0,1:S(1)} fusion(f32[128,2048]{0,1:T(8,128)S(1)} %bitcast.55, s32[128]{0:T(128)S(1)} %iota_add_fusion.2), kind=kOutput, calls=%fused_computation.40 | convolution fusion | flops 402817024 | bytes 2097664
  2.6 4.7 %slice_bitcast_fusion = (f32[1,4,16,8,64]{2,4,3,1,0:T(8,128)}, f32[1,4,16,8,64]{2,4,3,1,0:T(8,128)}, f32[1,4,16,8,64]{2,4,3,1,0:T(8,128)}, f32[1,4,16,8,64]{2,4,...) fusion(f32[4,128,8,64]{1,3,2,0:T(8,128)S(1)} %bitcast.56), kind=kLoop, calls=%fused_computation.4 | loop fusion | bytes 2097152 | tf_op jit(solution)/shard_map/stack | solution.py:29
  7.2 1.6 %copy.22 = f32[1,4,16,8,64]{4,3,2,1,0:T(8,128)S(1)} copy(f32[1,4,16,8,64]{2,4,3,1,0:T(8,128)} %get-tuple-element.5) | data formatting | bytes 262144 | tf_op jit(solution)/shard_map/stack | solution.py:29
  8.8 2.3 %copy.21 = f32[1,4,16,8,64]{4,3,2,1,0:T(8,128)} copy(f32[1,4,16,8,64]{2,4,3,1,0:T(8,128)} %get-tuple-element.6) | data formatting | bytes 262144 | tf_op jit(solution)/shard_map/stack | solution.py:29
  11.0 2.2 %copy.20 = f32[1,4,16,8,64]{4,3,2,1,0:T(8,128)} copy(f32[1,4,16,8,64]{2,4,3,1,0:T(8,128)} %get-tuple-element.7) | data formatting | bytes 262144 | tf_op jit(solution)/shard_map/stack | solution.py:29
  13.3 2.3 %copy.19 = f32[1,4,16,8,64]{4,3,2,1,0:T(8,128)} copy(f32[1,4,16,8,64]{2,4,3,1,0:T(8,128)} %get-tuple-element.8) | data formatting | bytes 262144 | tf_op jit(solution)/shard_map/stack | solution.py:29
  15.5 2.3 %copy.18 = f32[1,4,16,8,64]{4,3,2,1,0:T(8,128)} copy(f32[1,4,16,8,64]{2,4,3,1,0:T(8,128)} %get-tuple-element.9) | data formatting | bytes 262144 | tf_op jit(solution)/shard_map/stack | solution.py:29
  17.8 2.2 %copy.17 = f32[1,4,16,8,64]{4,3,2,1,0:T(8,128)} copy(f32[1,4,16,8,64]{2,4,3,1,0:T(8,128)} %get-tuple-element.10) | data formatting | bytes 262144 | tf_op jit(solution)/shard_map/stack | solution.py:29
  20.0 1.0 copy.16
  21.1 1.0 copy.15
  22.1 1.0 constant_dynamic-update-slice_fusion.7
  23.1 1.0 constant_dynamic-update-slice_fusion.6
  24.1 1.0 constant_dynamic-update-slice_fusion.5
  25.1 1.0 constant_dynamic-update-slice_fusion.4
  26.2 2.1 %reshape.80 = f32[8,1,32768]{2,1,0:T(1,128)} reshape(f32[8,4,16,8,64]{4,3,2,1,0:T(8,128)S(1)} %constant_dynamic-update-slice_fusion) | data formatting | bytes 2097152
  28.3 4.3 %all-to-all-start = ((f32[8,1,32768]{2,1,0:T(1,128)}), f32[8,1,32768]{2,1,0:T(1,128)S(1)}, u32[]{:S(2)}, u32[]{:S(2)}) async-start(f32[8,1,32768]{2,1,0:T(1,128)} %reshape.80), calls=%async_computation | async-start | bytes 2097152 | tf_op jit(solution)/shard_map/all_to_all | solution.py:28
  32.6 13.9 %all-to-all-done = f32[8,1,32768]{2,1,0:T(1,128)S(1)} async-done(((f32[8,1,32768]{2,1,0:T(1,128)}), f32[8,1,32768]{2,1,0:T(1,128)S(1)}, u32[]{:S(2)}, u32[]{:S(2)}) %all-to-all-start) | async-done | bytes 1048608 | tf_op jit(solution)/shard_map/all_to_all | solution.py:28
  47.0 4.5 %reduce = f32[8,32768]{1,0:T(8,128)} reduce(f32[8,1,32768]{2,1,0:T(1,128)S(1)} %all-to-all-done, f32[]{:T(128)} %broadcast.101), dimensions={1}, to_apply=%all_to_all.16.reduce_sub_computation | reduce | bytes 2097156 | tf_op jit(solution)/shard_map/all_to_all | solution.py:28
  51.5 2.1 %reshape.81 = f32[8,4,16,8,64]{4,3,2,1,0:T(8,128)S(1)} reshape(f32[8,32768]{1,0:T(8,128)} %reduce) | data formatting | bytes 2097152
  53.5 4.8 %fusion.3 = f32[4,16,64,64]{2,3,1,0:T(8,128)} fusion(f32[8,4,16,8,64]{4,3,2,1,0:T(8,128)S(1)} %reshape.81, s32[64]{0:T(128)S(1)} %iota_add_fusion.1), kind=kOutput, calls=%fused_computation.3 | convolution fusion | flops 201367552 | bytes 2097408 | tf_op jit(solution)/shard_map/dot_general | solution.py:18
  58.4 3.1 %copy.25 = f32[4,16,64,64]{3,1,0,2:T(8,128)S(1)} copy(f32[4,16,64,64]{2,3,1,0:T(8,128)} %fusion.3) | data formatting | bytes 2097152 | tf_op jit(solution)/shard_map/transpose | solution.py:21
  61.5 2.4 %reshape.82 = f32[4,1,65536]{2,1,0:T(1,128)} reshape(f32[64,4,16,64]{3,2,1,0:T(8,128)S(1)} %bitcast.57) | data formatting | bytes 2097152
  63.9 4.9 %all-to-all-start.1 = ((f32[4,1,65536]{2,1,0:T(1,128)}), f32[4,1,65536]{2,1,0:T(1,128)S(1)}, u32[]{:S(2)}, u32[]{:S(2)}) async-start(f32[4,1,65536]{2,1,0:T(1,128)} %reshape.82), calls=%async_computation.1 | async-start | bytes 2097152 | tf_op jit(solution)/shard_map/all_to_all | solution.py:35
  69.8 24.9 %all-to-all-done.1 = f32[4,1,65536]{2,1,0:T(1,128)S(1)} async-done(((f32[4,1,65536]{2,1,0:T(1,128)}), f32[4,1,65536]{2,1,0:T(1,128)S(1)}, u32[]{:S(2)}, u32[]{:S(2)}) %all-to-all-start.1) | async-done | bytes 1048608 | tf_op jit(solution)/shard_map/all_to_all | solution.py:35
  94.7 4.6 %reduce.1 = f32[4,65536]{1,0:T(4,128)} reduce(f32[4,1,65536]{2,1,0:T(1,128)S(1)} %all-to-all-done.1, f32[]{:T(128)} %broadcast.101), dimensions={1}, to_apply=%all_to_all.17.reduce_sub_computation | reduce | bytes 2097156 | tf_op jit(solution)/shard_map/all_to_all | solution.py:35
  99.4 2.2 %reshape.83 = f32[64,4,16,64]{3,2,1,0:T(8,128)S(1)} reshape(f32[4,65536]{1,0:T(4,128)} %reduce.1) | data formatting | bytes 2097152
  101.6 2.7 %copy.27 = f32[4,16,16,4,64]{4,3,2,1,0:T(4,128)} copy(f32[4,16,16,4,64]{4,1,0,2,3:T(8,128)S(1)} %bitcast.58) | data formatting | bytes 2097152 | tf_op jit(solution)/shard_map/all_to_all | solution.py:35
  104.3 2.5 %all_to_all.20 = f32[4,16,16,256]{3,2,1,0:T(8,128)S(1)} reshape(f32[4,16,16,4,64]{4,3,2,1,0:T(4,128)} %copy.27) | data formatting | bytes 2097152 | tf_op jit(solution)/shard_map/all_to_all | solution.py:35
  106.8 2.1 %fusion.13 = f32[4,16,16,256]{3,2,1,0:T(8,128)S(1)} fusion(f32[4,16,16,256]{3,2,1,0:T(8,128)S(1)} %all_to_all.20, s32[256]{0:T(256)S(1)} %iota_add_fusion), kind=kOutput, calls=%fused_computation.22 | convolution fusion | flops 805961728 | bytes 2098176 | tf_op jit(solution)/shard_map/dot_general | solution.py:18
  108.9 2.5 %fusion.6 = f32[16,16,256,4]{2,3,1,0:T(4,128)S(1)} fusion(f32[4,16,16,256]{3,2,1,0:T(8,128)S(1)} %fusion.13, f32[4,4]{1,0:T(4,128)S(1)} %copy-done.5), kind=kOutput, calls=%fused_computation.14 | convolution fusion | flops 12582912 | bytes 2097216 | tf_op jit(solution)/shard_map/ab,bxyz->axyz/dot_general | solution.py:43
  111.4 1.3 %bitcast_add_fusion = f32[4,16,16,256]{3,2,1,0:T(8,128)} fusion(f32[16,16,256,4]{2,3,1,0:T(4,128)S(1)} %fusion.6, f32[4,16,16,256]{3,2,1,0:T(8,128)S(1)} %fusion.13, f32[16,16,256]{2,1,0:T(8,128)S(1)} %copy-done.1, f32[16,16,256]{2,1,0:T(8,128)S(1)} %get-tuple-element.13), kind=kLoop, calls=%fused_computation.12 | loop fusion | flops 786432 | bytes 3670016 | tf_op jit(solution)/shard_map/add | solution.py:46
  (29 shorter events, 1.7 us)
Async XLA Ops:
  0.0 1.2 %copy-start = (f32[4,128,8,64]{1,3,2,0:T(8,128)S(1)}, f32[4,128,8,64]{1,3,2,0:T(8,128)}, u32[]{:S(2)}) copy-start(f32[4,128,8,64]{1,3,2,0:T(8,128)} %param.5) | copy-start | bytes 3145732
  22.1 4.0 %copy-start.4 = (f32[1,4,16,8,64]{4,3,2,1,0:T(8,128)S(1)}, f32[1,4,16,8,64]{4,3,2,1,0:T(8,128)}, u32[]{:S(2)}) copy-start(f32[1,4,16,8,64]{4,3,2,1,0:T(8,128)} %copy.19) | copy-start | bytes 393220
  22.1 4.0 %copy-start.3 = (f32[1,4,16,8,64]{4,3,2,1,0:T(8,128)S(1)}, f32[1,4,16,8,64]{4,3,2,1,0:T(8,128)}, u32[]{:S(2)}) copy-start(f32[1,4,16,8,64]{4,3,2,1,0:T(8,128)} %copy.20) | copy-start | bytes 393220
  22.1 4.0 %copy-start.2 = (f32[1,4,16,8,64]{4,3,2,1,0:T(8,128)S(1)}, f32[1,4,16,8,64]{4,3,2,1,0:T(8,128)}, u32[]{:S(2)}) copy-start(f32[1,4,16,8,64]{4,3,2,1,0:T(8,128)} %copy.21) | copy-start | bytes 393220
  28.3 18.1 %all-to-all-start = ((f32[8,1,32768]{2,1,0:T(1,128)}), f32[8,1,32768]{2,1,0:T(1,128)S(1)}, u32[]{:S(2)}, u32[]{:S(2)}) async-start(f32[8,1,32768]{2,1,0:T(1,128)} %reshape.80), calls=%async_computation | async-start | bytes 2097152 | tf_op jit(solution)/shard_map/all_to_all | solution.py:28
  61.5 7.3 %copy-start.7 = (f32[64]{0:T(128)S(1)}, f32[64]{0:T(128)}, u32[]{:S(2)}) copy-start(f32[64]{0:T(128)} %param.8) | copy-start | bytes 772
  61.5 7.4 %copy-start.8 = (f32[128]{0:T(128)S(1)}, f32[128]{0:T(128)}, u32[]{:S(2)}) copy-start(f32[128]{0:T(128)} %param.7) | copy-start | bytes 1540
  61.5 7.5 %copy-start.6 = (f32[256]{0:T(256)S(1)}, f32[256]{0:T(256)}, u32[]{:S(2)}) copy-start(f32[256]{0:T(256)} %param.9) | copy-start | bytes 3076
  63.9 30.8 %all-to-all-start.1 = ((f32[4,1,65536]{2,1,0:T(1,128)}), f32[4,1,65536]{2,1,0:T(1,128)S(1)}, u32[]{:S(2)}, u32[]{:S(2)}) async-start(f32[4,1,65536]{2,1,0:T(1,128)} %reshape.82), calls=%async_computation.1 | async-start | bytes 2097152 | tf_op jit(solution)/shard_map/all_to_all | solution.py:35
  104.3 4.6 %copy-start.5 = (f32[4,4]{1,0:T(4,128)S(1)}, f32[4,4]{1,0:T(4,128)}, u32[]{:S(2)}) copy-start(f32[4,4]{1,0:T(4,128)} %param.6) | copy-start | bytes 196
  106.8 4.6 %copy-start.1 = (f32[16,16,256]{2,1,0:T(8,128)S(1)}, f32[16,16,256]{2,1,0:T(8,128)}, u32[]{:S(2)}) copy-start(f32[16,16,256]{2,1,0:T(8,128)} %get-tuple-element.14) | copy-start | bytes 786436
